TPU v7x, 512 devices: a whole 4x4x16 slice. The times are simulated.
512 devices in a mesh: gy: 128 (over y, z_lo, x), gz: 4 (over z_hi, core).
Axes of the slice: x: 4, y: 4, z: 16 (z_hi: 2, z_lo: 8; z = z_hi * 8 + z_lo), core: 2. Of those that a mesh axis runs over, the one named last changes fastest.
Arguments:
- fuel: float32 [2048, 16, 2048], P('gy', 'gz'), may hold values from -6 to 6
- oxidant: float32 [2048, 16, 2048], P('gy', 'gz'), may hold values from -6 to 6
- rate: float32 [2048, 16, 2048], P('gy', 'gz'), may hold values from 0.05 to 0.5
- velocity: float32 [3], replicated, may hold values from -0.3 to 0.3
- sketch_x: float32 [128, 2048], replicated, may hold values from -0.125 to 0.125
- sketch_y: float32 [128, 2048], replicated, may hold values from -0.125 to 0.125
Outputs:
- sketch: float32 [128, 2, 16, 128], P('gy', None, 'gz')
All inputs are finite; a program needn't handle non-finite values.
Results may differ from a plain program's by a relative error of at most 0.00014.
Values sent between devices are 32-bit elements; how exact they have to be, the bound alone decides.
A program may use at most 64 MiB of HBM per device.

v0:
```python
import jax
import jax.numpy as jnp
from jax import lax
from jax.sharding import PartitionSpec as P

STEPS = 2


def with_halo(shard, sides, width):
    edges = {}
    for axis, dim in sides:
        devices, length = (lax.axis_size(axis), shard.shape[dim])
        up = [(i, (i + 1) % devices) for i in range(devices - 1)]
        last = lax.slice_in_dim(shard, length - width, length, axis=dim)
        leading = lax.slice_in_dim(shard, 0, width, axis=dim)
        edges[dim] = (
            lax.ppermute(last, axis, up),
            lax.ppermute(leading, axis, [(b, a) for a, b in up]),
        )
    done = []
    for _, dim in sides:
        low, high = edges[dim]
        around = [(width, width) if d in done else (0, 0) for d in range(shard.ndim)]
        shard = jnp.concatenate([jnp.pad(low, around), shard, jnp.pad(high, around)], axis=dim)
        done.append(dim)
    return shard


def advance(padded, rate, velocity):
    core = padded[:, 1:-1, 1:-1, :]
    xpad = jnp.pad(core, ((0, 0), (0, 0), (0, 0), (1, 1)))
    east = xpad[..., 2:]
    west = xpad[..., :-2]
    north = padded[:, 2:, 1:-1, :]
    south = padded[:, :-2, 1:-1, :]
    upper = padded[:, 1:-1, 2:, :]
    lower = padded[:, 1:-1, :-2, :]
    lap = east + west + north + south + upper + lower - 6.0 * core
    adv = 0.5 * (
        velocity[0] * (east - west) + velocity[1] * (north - south) + velocity[2] * (upper - lower)
    )
    react = rate * core[0] * core[1]
    new_fuel = core[0] + 0.1 * lap[0] - adv[0] - react
    new_oxid = core[1] + 0.05 * lap[1] - adv[1] + react
    return jnp.stack([new_fuel, new_oxid])


def per_device(fuel, oxidant, rate, velocity, sketch_x, sketch_y):
    rows_local = fuel.shape[0]
    planes_local = fuel.shape[1]
    width_x = fuel.shape[2]
    fields = jnp.stack([fuel, oxidant])
    for step in range(STEPS):
        padded = with_halo(fields, (("gy", 1), ("gz", 2)), 1)
        fields = advance(padded, rate, velocity)
    flat = fields.reshape(-1, width_x)
    projected = lax.dot_general(
        sketch_x, flat, (((1,), (1,)), ((), ())), precision=lax.Precision.HIGHEST
    )
    projected = projected.reshape(sketch_x.shape[0], 2, rows_local, planes_local)
    moved = lax.all_to_all(projected, "gy", split_axis=0, concat_axis=2, tiled=True)
    return jnp.einsum("kfyz,jy->kfzj", moved, sketch_y, precision=lax.Precision.HIGHEST)


def solution(mesh):
    in_specs = (P("gy", "gz", None), P("gy", "gz", None), P("gy", "gz", None), P(), P(), P())
    out_specs = P("gy", None, "gz", None)
    return jax.shard_map(
        per_device, mesh=mesh, in_specs=in_specs, out_specs=out_specs, check_vma=False
    )
```

profile of v0, /device:TPU:1, one launch (start us, length us, event | category | flops | bytes accessed | tf_op | source)
XLA Modules:
  0.0 123.4 jit_solution(6107158139650019086)
XLA Ops:
  0.0 1.0 fusion.30
  1.0 1.3 %collective-permute-start = (f32[2,1,4,2048]{3,2,1,0:T(4,128)S(1)}, f32[2,1,4,2048]{3,2,1,0:T(4,128)S(1)}, u32[]{:S(2)}, u32[]{:S(2)}) collective-permute-start(f32[2,1,4,2048]{3,2,1,0:T(4,128)S(1)} %get-tuple-element.16), channel_id=1, source_target_pairs={{4,0},{8,4},{12,8},{16,12},{20,16},{24,20},{28,24},{32,28},{36,32}... | collective-permute-start | bytes 196616 | tf_op jit(solution)/shard_map/ppermute | solution.py:18
  2.3 4.6 %collective-permute-start.1 = (f32[2,1,4,2048]{3,2,1,0:T(4,128)S(1)}, f32[2,1,4,2048]{3,2,1,0:T(4,128)S(1)}, u32[]{:S(2)}, u32[]{:S(2)}) collective-permute-start(f32[2,1,4,2048]{3,2,1,0:T(4,128)S(1)} %get-tuple-element.15), channel_id=1, source_target_pairs={{0,4},{4,8},{8,12},{12,16},{16,20},{20,24},{24,28},{28,32},{32,36}... | collective-permute-start | bytes 196616 | tf_op jit(solution)/shard_map/ppermute | solution.py:17
  6.9 0.4 fusion.25
  7.3 16.8 %collective-permute-start.3 = (f32[2,16,1,2048]{3,2,1,0:T(1,128)S(1)}, f32[2,16,1,2048]{3,2,1,0:T(1,128)S(1)}, u32[]{:S(2)}, u32[]{:S(2)}) collective-permute-start(f32[2,16,1,2048]{3,2,1,0:T(1,128)S(1)} %get-tuple-element.14), channel_id=1, source_target_pairs={{0,1},{1,2},{2,3},{4,5},{5,6},{6,7},{8,9},{9,10},{10,11},{12,13},{... | collective-permute-start | bytes 786440 | tf_op jit(solution)/shard_map/ppermute | solution.py:17
  24.1 1.9 %collective-permute-start.2 = (f32[2,16,1,2048]{3,2,1,0:T(1,128)S(1)}, f32[2,16,1,2048]{3,2,1,0:T(1,128)S(1)}, u32[]{:S(2)}, u32[]{:S(2)}) collective-permute-start(f32[2,16,1,2048]{3,2,1,0:T(1,128)S(1)} %get-tuple-element.13), channel_id=1, source_target_pairs={{1,0},{2,1},{3,2},{5,4},{6,5},{7,6},{9,8},{10,9},{11,10},{13,12},{... | collective-permute-start | bytes 786440 | tf_op jit(solution)/shard_map/ppermute | solution.py:18
  26.1 0.4 pad_maximum_fusion
  26.5 0.7 fusion.31
  27.4 18.9 %collective-permute-done.2 = f32[2,16,1,2048]{3,2,1,0:T(1,128)S(1)} collective-permute-done((f32[2,16,1,2048]{3,2,1,0:T(1,128)S(1)}, f32[2,16,1,2048]{3,2,1,0:T(1,128)S(1)}, u32[]{:S(2)}, u32[]{:S(2)}) %collective-permute-start.2) | collective-permute-done | bytes 262176 | tf_op jit(solution)/shard_map/ppermute | solution.py:18
  46.3 2.3 %multiply_subtract_fusion.1 = f32[2,16,4,2048]{3,2,1,0:T(4,128)S(1)} fusion(f32[2,16,4,2048]{3,2,1,0:T(4,128)S(1)} %pad_maximum_fusion, f32[2,1,4,2048]{3,2,1,0:T(4,128)S(1)} %collective-permute-done, f32[1,16,4,2048]{3,2,1,0:T(4,128)S(1)} %bitcast.98, f32[1,16,4,2048]{3,2,1,0:T(4,128)S(1)} %bitcast.103, f32[2,1,4,2048]{3,2,1,0:T(4,128)S(1)} %collective-permute-done.1, ...), kind=kLoop, calls=%fused_computation.54 | loop fusion | flops 6553600 | bytes 3801088 | tf_op jit(solution)/shard_map/sub | solution.py:38
  48.6 4.5 %add_multiply_fusion.1 = f32[2,16,4,2048]{3,2,1,0:T(4,128)S(1)} fusion(f32[2,16,4,2048]{3,2,1,0:T(4,128)S(1)} %pad_maximum_fusion, f32[]{:T(128)} %bitcast.5, f32[]{:T(128)} %bitcast.4, f32[]{:T(128)} %bitcast.3, f32[2,1,4,2048]{3,2,1,0:T(4,128)S(1)} %collective-permute-done, f32[1,16,4,2048]{3,2,1,0:T(4,128)S(1)} %bitcast.99, ...), kind=kLoop, calls=%fused_computation.53 | loop fusion | flops 7077888 | bytes 3801100 | tf_op jit(solution)/shard_map/mul | solution.py:39
  53.1 1.0 fusion.20
  54.1 0.4 fusion.23
  54.5 1.9 %collective-permute-start.7 = (f32[2,16,1,2048]{3,2,1,0:T(1,128)S(1)}, f32[2,16,1,2048]{3,2,1,0:T(1,128)S(1)}, u32[]{:S(2)}, u32[]{:S(2)}) collective-permute-start(f32[2,16,1,2048]{3,2,1,0:T(1,128)S(1)} %get-tuple-element.10), channel_id=1, source_target_pairs={{0,1},{1,2},{2,3},{4,5},{5,6},{6,7},{8,9},{9,10},{10,11},{12,13},{... | collective-permute-start | bytes 786440 | tf_op jit(solution)/shard_map/ppermute | solution.py:17
  56.4 2.4 %collective-permute-start.6 = (f32[2,16,1,2048]{3,2,1,0:T(1,128)S(1)}, f32[2,16,1,2048]{3,2,1,0:T(1,128)S(1)}, u32[]{:S(2)}, u32[]{:S(2)}) collective-permute-start(f32[2,16,1,2048]{3,2,1,0:T(1,128)S(1)} %get-tuple-element.9), channel_id=1, source_target_pairs={{1,0},{2,1},{3,2},{5,4},{6,5},{7,6},{9,8},{10,9},{11,10},{13,12},{... | collective-permute-start | bytes 786440 | tf_op jit(solution)/shard_map/ppermute | solution.py:18
  58.9 1.3 %collective-permute-start.4 = (f32[2,1,4,2048]{3,2,1,0:T(4,128)S(1)}, f32[2,1,4,2048]{3,2,1,0:T(4,128)S(1)}, u32[]{:S(2)}, u32[]{:S(2)}) collective-permute-start(f32[2,1,4,2048]{3,2,1,0:T(4,128)S(1)} %get-tuple-element.12), channel_id=1, source_target_pairs={{4,0},{8,4},{12,8},{16,12},{20,16},{24,20},{28,24},{32,28},{36,32}... | collective-permute-start | bytes 196616 | tf_op jit(solution)/shard_map/ppermute | solution.py:18
  60.2 4.0 %collective-permute-start.5 = (f32[2,1,4,2048]{3,2,1,0:T(4,128)S(1)}, f32[2,1,4,2048]{3,2,1,0:T(4,128)S(1)}, u32[]{:S(2)}, u32[]{:S(2)}) collective-permute-start(f32[2,1,4,2048]{3,2,1,0:T(4,128)S(1)} %get-tuple-element.11), channel_id=1, source_target_pairs={{0,4},{4,8},{8,12},{12,16},{16,20},{20,24},{24,28},{28,32},{32,36}... | collective-permute-start | bytes 196616 | tf_op jit(solution)/shard_map/ppermute | solution.py:17
  64.2 0.4 pad_maximum_fusion.1
  64.6 1.4 %collective-permute-done.5 = f32[2,1,4,2048]{3,2,1,0:T(4,128)S(1)} collective-permute-done((f32[2,1,4,2048]{3,2,1,0:T(4,128)S(1)}, f32[2,1,4,2048]{3,2,1,0:T(4,128)S(1)}, u32[]{:S(2)}, u32[]{:S(2)}) %collective-permute-start.5) | collective-permute-done | bytes 65568 | tf_op jit(solution)/shard_map/ppermute | solution.py:17
  65.9 10.8 %collective-permute-done.6 = f32[2,16,1,2048]{3,2,1,0:T(1,128)S(1)} collective-permute-done((f32[2,16,1,2048]{3,2,1,0:T(1,128)S(1)}, f32[2,16,1,2048]{3,2,1,0:T(1,128)S(1)}, u32[]{:S(2)}, u32[]{:S(2)}) %collective-permute-start.6) | collective-permute-done | bytes 262176 | tf_op jit(solution)/shard_map/ppermute | solution.py:18
  76.8 4.4 %add_multiply_fusion = f32[2,16,4,2048]{3,2,1,0:T(4,128)S(1)} fusion(f32[2,16,4,2048]{3,2,1,0:T(4,128)S(1)} %pad_maximum_fusion.1, f32[]{:T(128)} %bitcast.5, f32[]{:T(128)} %bitcast.4, f32[]{:T(128)} %bitcast.3, f32[2,1,4,2048]{3,2,1,0:T(4,128)S(1)} %collective-permute-done.4, f32[1,16,4,2048]{3,2,1,0:T(4,128)S(1)} %bitcast.93, ...), kind=kLoop, calls=%fused_computation.51 | loop fusion | flops 7077888 | bytes 3801100 | tf_op jit(solution)/shard_map/mul | solution.py:39
  81.2 2.3 %multiply_subtract_fusion = f32[2,16,4,2048]{3,2,1,0:T(4,128)S(1)} fusion(f32[2,16,4,2048]{3,2,1,0:T(4,128)S(1)} %pad_maximum_fusion.1, f32[2,1,4,2048]{3,2,1,0:T(4,128)S(1)} %collective-permute-done.4, f32[1,16,4,2048]{3,2,1,0:T(4,128)S(1)} %bitcast.94, f32[1,16,4,2048]{3,2,1,0:T(4,128)S(1)} %bitcast.89, f32[2,1,4,2048]{3,2,1,0:T(4,128)S(1)} %collective-permute-done.5, ...), kind=kLoop, calls=%fused_computation.52 | loop fusion | flops 6553600 | bytes 3801088 | tf_op jit(solution)/shard_map/sub | solution.py:38
  83.5 1.0 fusion.12
  84.7 0.4 reshape.19
  85.1 1.0 fusion.32
  86.4 0.4 reshape.23
  86.8 31.9 %all_to_all.15 = f32[128,1,128]{2,1,0:T(1,128)S(1)} all-to-all(f32[128,1,128]{2,1,0:T(1,128)S(1)} %reshape.23), channel_id=1, replica_groups=mesh['gy'=128,'gz'=4] {'gy'}, dimensions={0} | all-to-all | bytes 131072 | tf_op jit(solution)/shard_map/all_to_all | solution.py:61
  118.8 0.5 broadcast.122
  119.3 0.8 reduce
  120.1 0.4 reshape.24
  120.9 0.8 copy-done.4
  121.7 1.6 %convolution_bitcast_fusion = f32[1,2,4,128]{3,2,1,0:T(4,128)} fusion(f32[2,2048,4]{1,2,0:T(4,128)S(1)} %reshape.21, f32[128,2048]{1,0:T(8,128)S(1)} %copy-done.4), kind=kOutput, calls=%fused_computation.18 | convolution fusion | flops 25165824 | bytes 1118208 | tf_op jit(solution)/shard_map/kfyz,jy->kfzj/dot_general | solution.py:62
  (22 shorter events, 1.3 us)
Async XLA Ops:
  0.0 85.1 %copy-start = (f32[128,2048]{1,0:T(8,128)S(1)}, f32[128,2048]{1,0:T(8,128)}, u32[]{:S(2)}) copy-start(f32[128,2048]{1,0:T(8,128)} %param.10) | copy-start | bytes 3145732
  0.0 6.9 %copy-start.1 = (f32[16,4,2048]{2,1,0:T(4,128)S(1)}, f32[16,4,2048]{2,1,0:T(4,128)}, u32[]{:S(2)}) copy-start(f32[16,4,2048]{2,1,0:T(4,128)} %param.7) | copy-start | bytes 1572868
  0.0 6.9 %copy-start.2 = (f32[16,4,2048]{2,1,0:T(4,128)S(1)}, f32[16,4,2048]{2,1,0:T(4,128)}, u32[]{:S(2)}) copy-start(f32[16,4,2048]{2,1,0:T(4,128)} %param.6) | copy-start | bytes 1572868
  1.0 26.1 %collective-permute-start = (f32[2,1,4,2048]{3,2,1,0:T(4,128)S(1)}, f32[2,1,4,2048]{3,2,1,0:T(4,128)S(1)}, u32[]{:S(2)}, u32[]{:S(2)}) collective-permute-start(f32[2,1,4,2048]{3,2,1,0:T(4,128)S(1)} %get-tuple-element.16), channel_id=1, source_target_pairs={{4,0},{8,4},{12,8},{16,12},{20,16},{24,20},{28,24},{32,28},{36,32}... | collective-permute-start | bytes 196616 | tf_op jit(solution)/shard_map/ppermute | solution.py:18
  2.3 24.8 %collective-permute-start.1 = (f32[2,1,4,2048]{3,2,1,0:T(4,128)S(1)}, f32[2,1,4,2048]{3,2,1,0:T(4,128)S(1)}, u32[]{:S(2)}, u32[]{:S(2)}) collective-permute-start(f32[2,1,4,2048]{3,2,1,0:T(4,128)S(1)} %get-tuple-element.15), channel_id=1, source_target_pairs={{0,4},{4,8},{8,12},{12,16},{16,20},{20,24},{24,28},{28,32},{32,36}... | collective-permute-start | bytes 196616 | tf_op jit(solution)/shard_map/ppermute | solution.py:17
  7.3 20.1 %collective-permute-start.3 = (f32[2,16,1,2048]{3,2,1,0:T(1,128)S(1)}, f32[2,16,1,2048]{3,2,1,0:T(1,128)S(1)}, u32[]{:S(2)}, u32[]{:S(2)}) collective-permute-start(f32[2,16,1,2048]{3,2,1,0:T(1,128)S(1)} %get-tuple-element.14), channel_id=1, source_target_pairs={{0,1},{1,2},{2,3},{4,5},{5,6},{6,7},{8,9},{9,10},{10,11},{12,13},{... | collective-permute-start | bytes 786440 | tf_op jit(solution)/shard_map/ppermute | solution.py:17
  24.1 2.3 %copy-start.5 = (f32[3]{0:T(128)S(1)}, f32[3]{0:T(128)}, u32[]{:S(2)}) copy-start(f32[3]{0:T(128)} %param.9) | copy-start | bytes 40
  24.1 22.1 %collective-permute-start.2 = (f32[2,16,1,2048]{3,2,1,0:T(1,128)S(1)}, f32[2,16,1,2048]{3,2,1,0:T(1,128)S(1)}, u32[]{:S(2)}, u32[]{:S(2)}) collective-permute-start(f32[2,16,1,2048]{3,2,1,0:T(1,128)S(1)} %get-tuple-element.13), channel_id=1, source_target_pairs={{1,0},{2,1},{3,2},{5,4},{6,5},{7,6},{9,8},{10,9},{11,10},{13,12},{... | collective-permute-start | bytes 786440 | tf_op jit(solution)/shard_map/ppermute | solution.py:18
  48.6 4.5 %copy-start.3 = (f32[16,4,2048]{2,1,0:T(4,128)S(1)}, f32[16,4,2048]{2,1,0:T(4,128)}, u32[]{:S(2)}) copy-start(f32[16,4,2048]{2,1,0:T(4,128)} %param.8) | copy-start | bytes 1572868
  54.5 11.5 %collective-permute-start.7 = (f32[2,16,1,2048]{3,2,1,0:T(1,128)S(1)}, f32[2,16,1,2048]{3,2,1,0:T(1,128)S(1)}, u32[]{:S(2)}, u32[]{:S(2)}) collective-permute-start(f32[2,16,1,2048]{3,2,1,0:T(1,128)S(1)} %get-tuple-element.10), channel_id=1, source_target_pairs={{0,1},{1,2},{2,3},{4,5},{5,6},{6,7},{8,9},{9,10},{10,11},{12,13},{... | collective-permute-start | bytes 786440 | tf_op jit(solution)/shard_map/ppermute | solution.py:17
  56.4 20.4 %collective-permute-start.6 = (f32[2,16,1,2048]{3,2,1,0:T(1,128)S(1)}, f32[2,16,1,2048]{3,2,1,0:T(1,128)S(1)}, u32[]{:S(2)}, u32[]{:S(2)}) collective-permute-start(f32[2,16,1,2048]{3,2,1,0:T(1,128)S(1)} %get-tuple-element.9), channel_id=1, source_target_pairs={{1,0},{2,1},{3,2},{5,4},{6,5},{7,6},{9,8},{10,9},{11,10},{13,12},{... | collective-permute-start | bytes 786440 | tf_op jit(solution)/shard_map/ppermute | solution.py:18
  58.9 5.7 %collective-permute-start.4 = (f32[2,1,4,2048]{3,2,1,0:T(4,128)S(1)}, f32[2,1,4,2048]{3,2,1,0:T(4,128)S(1)}, u32[]{:S(2)}, u32[]{:S(2)}) collective-permute-start(f32[2,1,4,2048]{3,2,1,0:T(4,128)S(1)} %get-tuple-element.12), channel_id=1, source_target_pairs={{4,0},{8,4},{12,8},{16,12},{20,16},{24,20},{28,24},{32,28},{36,32}... | collective-permute-start | bytes 196616 | tf_op jit(solution)/shard_map/ppermute | solution.py:18
  60.2 5.8 %collective-permute-start.5 = (f32[2,1,4,2048]{3,2,1,0:T(4,128)S(1)}, f32[2,1,4,2048]{3,2,1,0:T(4,128)S(1)}, u32[]{:S(2)}, u32[]{:S(2)}) collective-permute-start(f32[2,1,4,2048]{3,2,1,0:T(4,128)S(1)} %get-tuple-element.11), channel_id=1, source_target_pairs={{0,4},{4,8},{8,12},{12,16},{16,20},{20,24},{24,28},{28,32},{32,36}... | collective-permute-start | bytes 196616 | tf_op jit(solution)/shard_map/ppermute | solution.py:17
  120.5 1.2 copy-start.4
where the time goes:
time: 124 us; the launch traced here: 123 us
  starting transfers between devices  34.2 us (28%)
  blocking collectives  31.9 us (26%)
  waiting for transfers between devices  31.4 us (25%)
  other arithmetic  19.1 us (15%)
  local copies, waits for them, and re-layouts  3.88 us (3%)
  matrix products  2.6 us (2%)
    all_to_all x1, blocking collectives, per_device(): lax.all_to_all(projected, 'gy', split_axis=0, concat_axis=2, tiled=True)  31.9 us
    ppermute x4, waiting for transfers between devices, with_halo(): lax.ppermute(leading, axis, [(b, a) for a, b in up])  29.7 us
    ppermute x4, starting transfers between devices, with_halo(): lax.ppermute(last, axis, up)  27.3 us
    mul x2, other arithmetic, advance(): 0.5 * (velocity[0] * (east - west) + velocity[1] * (north - south) + velo...  8.86 us
    ppermute x4, starting transfers between devices, with_halo(): lax.ppermute(leading, axis, [(b, a) for a, b in up])  6.92 us
    sub x2, other arithmetic, advance(): lap = east + west + north + south + upper + lower - 6.0 * core  4.64 us
  transfers between devices with their start and end apart: 8, of which 4 were waited for; matrix products, arithmetic and copies ran while one was open for 2% of the time, Pallas kernels for 0%

commit v1 on v0

v1 whole, which is shorter than its diff:
```python
import functools

import jax
import jax.numpy as jnp
from jax import lax
from jax.experimental import pallas as pl
from jax.experimental.pallas import tpu as pltpu
from jax.sharding import PartitionSpec as P

F32, BF16 = jnp.float32, jnp.bfloat16
MESH = pl.DeviceIdType.MESH
NX, NZL, NY = 4, 8, 4
DEVS = NX * NZL * NY
NT = 16
ROWS = 16


def roll(v, shift, axis):
    shift %= v.shape[axis]
    return pltpu.roll(v, shift, axis) if shift else v


def split(v):
    high = v.astype(BF16)
    return high, (v - high.astype(F32)).astype(BF16)


def dot(a, b, dims):
    return lax.dot_general(a, b, (dims, ((), ())), preferred_element_type=F32)


def kernel(
    fuel, fuel4, oxid, oxid4, rate, vel, sx, sy, out,
    F, RR, HB, VB, UF, RC, CC, CG, LT, SX, SXH, SXL, SY, SYT, SYH, SYL,
    P1, ZD, PC, ZC, EA, ER, TA, TR, AE,
    s_vb, s_f, s_rr, s_sx, s_sy, far_s, far_r, ys, yr, ds, dr, zd_s, zd_r, zc_s, zc_r, ea_s, ea_r, ta_s, ta_r,
    x1, x2, y1, y2, zu, zd, go,
):
    gy, gz = lax.axis_index("gy"), lax.axis_index("gz")
    x, zl, y = gy % NX, (gy // NX) % NZL, gy // (NX * NZL)
    core = gz % 2
    inner = (gz == 1) | (gz == 2)
    rim = jnp.logical_not(inner)
    partner = {"gy": gy, "gz": gz + 1 - 2 * core}
    opposite = {"gy": gy, "gz": 3 - gz}

    def at(yy, zz, xx):
        return {"gy": (yy * NZL + zz) * NX + xx, "gz": gz}

    def signal(sem, device):
        pl.semaphore_signal(sem, inc=1, device_id=device, device_id_type=MESH)

    def remote(src, dst, send, recv, device):
        return pltpu.make_async_remote_copy(
            src_ref=src, dst_ref=dst, send_sem=send, recv_sem=recv, device_id=device, device_id_type=MESH
        )

    def plane(p):
        return p + core * (3 - 2 * p)

    for f, src in enumerate((fuel4, oxid4)):
        for j in range(4):
            pltpu.make_async_copy(src.at[:, j, :, plane(0), :], VB.at[:, :, f * 4 + j, :], s_vb).start()
    for f, src in enumerate((fuel, oxid)):
        for p in (3, 0, 1, 2):
            pltpu.make_async_copy(src.at[:, :, plane(p), :], F.at[pl.ds(1, ROWS), :, f * 4 + p, :], s_f).start()
    for p in range(4):
        for f in range(2):
            pltpu.make_async_copy(rate.at[:, :, plane(p), :], RR.at[:, :, f * 4 + p, :], s_rr).start()
    pltpu.make_async_copy(sx, SX, s_sx).start()
    pltpu.make_async_copy(sy, SY, s_sy).start()

    barrier = pltpu.get_barrier_semaphore()
    signal(barrier, partner)
    right, left = at(y, zl, (x + 1) % NX), at(y, zl, (x + NX - 1) % NX)
    front, back = at((y + 1) % NY, zl, x), at((y + NY - 1) % NY, zl, x)
    above, below = at(y, zl + 1, x), at(y, zl - 1, x)

    @pl.when(inner)
    def _():
        signal(barrier, opposite)

    @pl.when(rim)
    def _():
        for device in (right, left, front, back):
            signal(barrier, device)

        @pl.when(zl < NZL - 1)
        def _():
            signal(barrier, above)

        @pl.when(zl > 0)
        def _():
            signal(barrier, below)

        UF[...] = jnp.zeros_like(UF)
        ZC[...] = jnp.zeros_like(ZC)

    @pl.when(gy == 0)
    def _():
        F[0] = jnp.zeros((NT, 8, 128), F32)

    @pl.when(gy == DEVS - 1)
    def _():
        F[ROWS + 1] = jnp.zeros((NT, 8, 128), F32)

    @pl.when(inner)
    def _():
        pl.semaphore_wait(barrier, 2)

    @pl.when(rim & ((zl == 0) | (zl == NZL - 1)))
    def _():
        pl.semaphore_wait(barrier, 6)

    @pl.when(rim & (zl > 0) & (zl < NZL - 1))
    def _():
        pl.semaphore_wait(barrier, 7)

    def far(g):
        return remote(VB.at[g], UF.at[g], far_s.at[g], far_r.at[g], opposite)

    pltpu.make_async_copy(VB, VB, s_vb).wait()

    @pl.when(inner)
    def _():
        for g in range(4):
            far(g).start()

    def deck(f):
        return remote(
            F.at[pl.ds(1, ROWS), :, f * 4 + 3, :], HB.at[:, :, f * 4 + 3, :], ds.at[f], dr.at[f], partner
        )

    pltpu.make_async_copy(F.at[pl.ds(1, ROWS)], F.at[pl.ds(1, ROWS)], s_f).wait()
    for f in range(2):
        deck(f).start()

    @pl.when(rim)
    def _():
        signal(x1, right)
        signal(x1, left)
        pl.semaphore_wait(x1, 2)
        signal(x2, right)
        pl.semaphore_wait(x2, 1)
        signal(y1, front)
        signal(y1, back)
        pl.semaphore_wait(y1, 2)
        signal(y2, front)
        pl.semaphore_wait(y2, 1)

        @pl.when(zl == 0)
        def _():
            signal(zu, above)

        @pl.when(zl == NZL - 1)
        def _():
            signal(zd, below)

        @pl.when((zl > 0) & (zl < NZL // 2))
        def _():
            pl.semaphore_wait(zu, 1)
            signal(zu, above)
            pl.semaphore_wait(zd, 1)
            signal(zd, below)

        @pl.when((zl < NZL - 1) & (zl >= NZL // 2))
        def _():
            pl.semaphore_wait(zd, 1)
            signal(zd, below)
            pl.semaphore_wait(zu, 1)
            signal(zu, above)

        @pl.when(zl == 0)
        def _():
            pl.semaphore_wait(zd, 1)

        @pl.when(zl == NZL - 1)
        def _():
            pl.semaphore_wait(zu, 1)

        signal(go, partner)

    sub = lax.broadcasted_iota(jnp.int32, (8, 128), 0)
    lane = lax.broadcasted_iota(jnp.int32, (8, 128), 1)
    sp = sub % 4
    v0, v1 = 0.5 * vel[0], 0.5 * vel[1]
    v2 = 0.5 * vel[2] * (1 - 2 * core).astype(F32)
    alpha = jnp.where(sub < 4, 0.1, 0.05).astype(F32)
    zero = jnp.zeros((8, 128), F32)
    k0, kE, kW, kN, kS = 1.0 - 6.0 * alpha, alpha - v0, alpha + v0, alpha - v1, alpha + v1
    kP, kM = alpha - v2, alpha + v2
    sg = jnp.where(sub < 4, -1.0, 1.0).astype(F32)
    kMz = jnp.where(sp == 0, zero, kM)
    kPz = jnp.where(sp == 3, zero, kP)
    sgm = jnp.where(sp == 0, zero, sg)
    first, last = lane == 0, lane == 127

    def along_x(row):
        east = [roll(v, 127, 1) for v in row] + [zero]
        west = [zero] + [roll(v, 1, 1) for v in row]
        return [
            k0 * row[t]
            + kE * jnp.where(last, east[t + 1], east[t])
            + kW * jnp.where(first, west[t], west[t + 1])
            for t in range(NT)
        ]

    def compact(four):
        v = four[0]
        for j in range(1, 4):
            v = jnp.where(sp == j, roll(four[j], j, 0), v)
        return v

    pltpu.make_async_copy(sx, SX, s_sx).wait()

    @pl.loop(0, 8)
    def _(i):
        rows = pl.ds(pl.multiple_of(i * 16, 16), 16)
        SXH[rows, :], SXL[rows, :] = split(SX[rows, :])

    pltpu.make_async_copy(sy, SY, s_sy).wait()
    for b in range(16):
        SYT[b * 128 : (b + 1) * 128, :] = SY[:, b * 128 : (b + 1) * 128].T
    for r in range(ROWS):
        rows = slice(r * 128, (r + 1) * 128)
        SYH[rows, :], SYL[rows, :] = split(SYT[pl.ds(r, 128, stride=16), :])

    def project(read, rows):
        total = jnp.zeros((rows, 128), F32)
        for c in range(NT // 2):
            high, low = split(jnp.concatenate([read(2 * c), read(2 * c + 1)], axis=1))
            cols = slice(c * 256, (c + 1) * 256)
            nt = ((1,), (1,))
            total += dot(high, SXH[:, cols], nt) + dot(low, SXH[:, cols], nt) + dot(high, SXL[:, cols], nt)
        return total

    P0 = project(lambda t: VB[:, t].reshape(32, 128), 32).reshape(4, 8, 128)

    @pl.when(inner)
    def _():
        pl.semaphore_wait(go, 1)

    north = {"gy": gy + 1, "gz": gz}
    south = {"gy": gy - 1, "gz": gz}

    def to_north():
        return remote(F.at[ROWS], F.at[0], ys.at[0], yr.at[0], north)

    def to_south():
        return remote(F.at[1], F.at[ROWS + 1], ys.at[1], yr.at[1], south)

    @pl.when(gy < DEVS - 1)
    def _():
        to_north().start()

    @pl.when(gy > 0)
    def _():
        to_south().start()

    pltpu.make_async_copy(RR, RR, s_rr).wait()
    for f in range(2):
        deck(f).wait_recv()

    @pl.when(gy > 0)
    def _():
        to_north().wait_recv()

    @pl.when(gy < DEVS - 1)
    def _():
        to_south().wait_recv()

    @pl.loop(0, ROWS)
    def _(r):
        row = [F[r + 1, t] for t in range(NT)]
        ahead = along_x(row)
        after = []
        for t in range(NT):
            v = row[t]
            up = jnp.where(sp == 3, HB[r, t], roll(v, 7, 0))
            c = ahead[t] + kN * F[r + 2, t] + kS * F[r, t] + kP * up + kMz * roll(v, 1, 0)
            c += sg * RR[r, t] * v * roll(v, 4, 0)
            CG[0, r, t] = c
            after.append(c)
        for t, g in enumerate(along_x(after)):
            c = after[t]
            CG[1, r, t] = g + sgm * RR[r, t] * c * roll(c, 4, 0)

    early = project(lambda t: CG[:, :, t].reshape(256, 128), 256)
    P1[...] = early[:128].reshape(ROWS, 8, 128)
    for g in range(4):
        PC[g] = compact([P1[4 * g + j] for j in range(4)])

    def to_partner():
        return remote(P1, ZD, zd_s, zd_r, partner)

    def to_opposite():
        return remote(PC, ZC, zc_s, zc_r, opposite)

    to_partner().start()

    @pl.when(inner)
    def _():
        to_opposite().start()

    Q = early[128:].reshape(ROWS, 8, 128)

    @pl.loop(0, 4)
    def _(g):
        for t in range(NT):
            CC[g, t] = compact([CG[0, 4 * g + j, t] for j in range(4)])
            RC[g, t] = compact([RR[4 * g + j, t] for j in range(4)])

    to_partner().wait_recv()
    rows = []
    for r in range(ROWS):
        v = P1[r]
        e = Q[r] + kPz * roll(v, 7, 0) + kMz * roll(v, 1, 0) + jnp.where(sp == 3, kP * ZD[r], zero)
        if r < ROWS - 1:
            e += kN * P1[r + 1]
        if r > 0:
            e += kS * P1[r - 1]
        rows.append(e)
    EA[...] = jnp.concatenate(rows, axis=0).T

    def exchange(src, dst, send, recv):
        @pl.loop(1, DEVS)
        def _(i):
            to = lax.rem(gy + i, DEVS)
            remote(src.at[pl.ds(to, 1), :], dst.at[pl.ds(gy, 1), :], send, recv, {"gy": to, "gz": gz}).start()

        dst[pl.ds(gy, 1), :] = src[pl.ds(gy, 1), :]

    def all_rows(src, dst, send, recv):
        return remote(src.at[pl.ds(0, DEVS - 1), :], dst.at[pl.ds(0, DEVS - 1), :], send, recv, partner)

    exchange(EA, ER, ea_s, ea_r)

    for g in range(4):
        @pl.when(inner)
        def _():
            far(g).wait_recv()

        delta = [kM * UF[g, t] for t in range(NT)]
        for t, q in enumerate(along_x(delta)):
            c = CC[g, t] + delta[t]
            LT[g, t] = delta[t]
            LT[4 + g, t] = q + sg * RC[g, t] * c * roll(c, 4, 0)
    late = project(lambda t: LT[:, t].reshape(64, 128), 64).reshape(8, 8, 128)

    @pl.when(inner)
    def _():
        to_opposite().wait_recv()

    kF = kM * kP * jnp.where(inner, 1.0, 0.0).astype(F32)
    D = [late[g] for g in range(4)]
    X = []
    for g in range(4):
        v = late[4 + g] + kF * P0[g] + kM * ZC[g]
        ahead = roll(D[g + 1], 3, 0) if g < 3 else zero
        behind = roll(D[g - 1], 5, 0) if g > 0 else zero
        v += kN * jnp.where(sp == 3, ahead, roll(D[g], 7, 0))
        v += kS * jnp.where(sp == 0, behind, roll(D[g], 1, 0))
        X.append(v)
    low_edge = kN * P1[0] + jnp.where(sp == 0, kN * D[0], zero)
    high_edge = kS * P1[ROWS - 1] + jnp.where(sp == 0, kS * roll(D[3], 5, 0), zero)
    spare = [low_edge, roll(low_edge, 2, 0), high_edge, roll(high_edge, 2, 0)] + [zero] * (ROWS - 4)
    rows = []
    for r in range(ROWS):
        g, j = divmod(r, 4)
        v = jnp.where(sp == 0, roll(X[g], 8 - j, 0), spare[r])
        rows.append(jnp.where(sp == 1, kM * roll(D[g], 9 - j, 0), v))
    TA[...] = jnp.concatenate(rows, axis=0).T
    exchange(TA, TR, ta_s, ta_r)

    all_rows(EA, ER, ea_s, ea_r).wait_recv()
    AE[...] = ER[...].T
    all_rows(TA, TR, ta_s, ta_r).wait_recv()
    T = TR[...].T
    tail = [T[8 * r : 8 * r + 8] for r in range(ROWS)]
    low_edge = jnp.where(sp >= 2, tail[0], roll(tail[1], 6, 0))
    high_edge = jnp.where(sp >= 2, tail[2], roll(tail[3], 6, 0))
    A = [AE[8 * r : 8 * r + 8, :] + jnp.where(sp < 2, tail[r], zero) for r in range(ROWS)]
    A[ROWS - 1] += jnp.where(last, zero, roll(low_edge, 127, 1))
    A[0] += jnp.where(first, zero, roll(high_edge, 1, 1))
    high, low = split(jnp.concatenate(A, axis=1))
    nn = ((1,), (0,))
    res = dot(high, SYH[...], nn) + dot(low, SYH[...], nn) + dot(high, SYL[...], nn)
    flipped = jnp.where(
        sp == 0, roll(res, 5, 0), jnp.where(sp == 1, roll(res, 7, 0), jnp.where(sp == 2, roll(res, 1, 0), roll(res, 3, 0)))
    )
    res = jnp.where(jnp.full((8, 128), core) == 1, flipped, res)
    out[0, 0] = res[:4]
    out[0, 1] = res[4:]

    @pl.when(inner)
    def _():
        for g in range(4):
            far(g).wait_send()
        to_opposite().wait_send()

    for f in range(2):
        deck(f).wait_send()

    @pl.when(gy < DEVS - 1)
    def _():
        to_north().wait_send()

    @pl.when(gy > 0)
    def _():
        to_south().wait_send()

    to_partner().wait_send()
    all_rows(EA, ER, ea_s, ea_r).wait_send()
    all_rows(TA, TR, ta_s, ta_r).wait_send()


def per_device(fuel, oxidant, rate, velocity, sketch_x, sketch_y):
    def tiles(a):
        return a.reshape(ROWS, 4, NT, 128).transpose(0, 2, 1, 3)

    def tiles4(a):
        return tiles(a).reshape(4, 4, NT, 4, 128)

    vm = lambda *shape, kind=F32: pltpu.VMEM(shape, kind)
    dma, one = pltpu.SemaphoreType.DMA, pltpu.SemaphoreType.REGULAR
    whole = (ROWS, NT, 8, 128)
    plane = (4, NT, 8, 128)
    return pl.pallas_call(
        kernel,
        out_shape=jax.ShapeDtypeStruct((1, 2, 4, 128), F32),
        in_specs=[pl.BlockSpec(memory_space=pl.ANY)] * 5
        + [pl.BlockSpec(memory_space=pltpu.SMEM)]
        + [pl.BlockSpec(memory_space=pl.ANY)] * 2,
        out_specs=pl.BlockSpec(memory_space=pltpu.VMEM),
        scratch_shapes=[
            vm(ROWS + 2, NT, 8, 128), vm(*whole), vm(*whole), vm(*plane), vm(*plane), vm(*plane), vm(*plane),
            vm(2, *whole), vm(8, NT, 8, 128), vm(128, 2048), vm(128, 2048, kind=BF16), vm(128, 2048, kind=BF16),
            vm(128, 2048), vm(2048, 128), vm(2048, 128, kind=BF16), vm(2048, 128, kind=BF16),
            vm(ROWS, 8, 128), vm(ROWS, 8, 128), vm(4, 8, 128), vm(4, 8, 128),
            vm(128, 128), vm(128, 128), vm(128, 128), vm(128, 128), vm(128, 128),
            dma, dma, dma, dma, dma, dma((4,)), dma((4,)), dma((2,)), dma((2,)), dma((2,)), dma((2,)),
            dma, dma, dma, dma, dma, dma, dma, dma,
            one, one, one, one, one, one, one,
        ],
        compiler_params=pltpu.CompilerParams(collective_id=0, has_side_effects=True),
        name="advect_sketch",
    )(tiles(fuel), tiles4(fuel), tiles(oxidant), tiles4(oxidant), tiles(rate), velocity, sketch_x, sketch_y)


def solution(mesh):
    in_specs = (P("gy", "gz", None), P("gy", "gz", None), P("gy", "gz", None), P(), P(), P())
    out_specs = P("gy", None, "gz", None)
    return jax.shard_map(per_device, mesh=mesh, in_specs=in_specs, out_specs=out_specs, check_vma=False)
```

time: 124 us -> 58.8 us (0.47)
  Pallas kernels: 0 us -> 57.4 us
  starting transfers between devices: 34.2 us -> 0 us
  blocking collectives: 31.9 us -> 0 us
  waiting for transfers between devices: 31.4 us -> 0 us
  other arithmetic: 19.1 us -> 0 us
  matrix products: 2.6 us -> 0 us
  local copies, waits for them, and re-layouts: 3.88 us -> 1.28 us
    pallas_call x0 -> x1, Pallas kernels: none -> 57.4 us  [per_device(): pl.pallas_call(kernel, out_shape=jax.ShapeDtypeStruct((1, 2, 4, 128), F32...]
    ppermute x8 -> x0, starting transfers between devices: 34.2 us -> none  [the longest x4 27.3 us: with_halo(): lax.ppermute(last, axis, up)]
    all_to_all x1 -> x0, blocking collectives: 31.9 us -> none  [per_device(): lax.all_to_all(projected, 'gy', split_axis=0, concat_axis=2, tiled=True)]
    ppermute x8 -> x0, waiting for transfers between devices: 31.4 us -> none  [the longest x4 29.7 us: with_halo(): lax.ppermute(leading, axis, [(b, a) for a, b in up])]
    mul x2 -> x0, other arithmetic: 8.86 us -> none  [advance(): 0.5 * (velocity[0] * (east - west) + velocity[1] * (north - south) + velo...]
    sub x3 -> x0, other arithmetic: 5.6 us -> none  [the longest x2 4.64 us: advance(): lap = east + west + north + south + upper + lower - 6.0 * core]
    another operation x8 -> x0, other arithmetic: 3.8 us -> none  [the longest x5 2.02 us: advance(): return jnp.stack([new_fuel, new_oxid])]
    dot_general x2 -> x0, matrix products: 2.6 us -> none  [the longest x1 1.61 us: per_device(): jnp.einsum('kfyz,jy->kfzj', moved, sketch_y, precision=lax.Precision.HIGH...]
  transfers between devices with their start and end apart: 8 -> 0, of which waited for: 4 -> 0; matrix products, arithmetic and copies ran while one was open for 2% -> 0% of each run, Pallas kernels for 0% -> 0%
where the time goes in v1:
time: 58.8 us; the launch traced here: 58.7 us
  Pallas kernels  57.4 us (98%)
  local copies, waits for them, and re-layouts  1.28 us (2%)
    pallas_call x1, Pallas kernels, per_device(): pl.pallas_call(kernel, out_shape=jax.ShapeDtypeStruct((1, 2, 4, 128), F32...  57.4 us
    unnamed x1, local copies, waits for them, and re-layouts  1.28 us

profile of v1, /device:TPU:1, one launch (start us, length us, event | category | flops | bytes accessed | tf_op | source)
XLA Modules:
  0.0 58.7 jit_solution(3451140722198165008)
XLA Ops:
  0.0 57.4 %advect_sketch.1 = f32[1,2,4,128]{3,2,1,0:T(4,128)} custom-call(f32[16,16,4,128]{3,2,1,0:T(4,128)} %bitcast.13, f32[4,4,16,4,128]{4,3,2,1,0:T(4,128)} %bitcast.14, f32[16,16,4,128]{3,2,1,0:T(4,128)} %bitcast.15, f32[4,4,16,4,128]{4,3,2,1,0:T(4,128)} %bitcast.16, f32[16,16,4,128]{3,2,1,0:T(4,128)} %bitcast.17, f32[3]{0:T(128)} %vel.1, f32[128,2048]{1,0:T(8,128)} %sx.1, ...), custom_call_target="tpu_custom_call" | custom-call | tf_op jit(solution)/shard_map/advect_sketch/pallas_call | solution.py:428
  57.4 1.3 %copy.8 = f32[1,2,4,128]{3,2,1,0:T(4,128)} copy(f32[1,2,4,128]{3,2,1,0:T(4,128)} %advect_sketch.1) | data formatting | bytes 8192

commit v2 on v1

--- a/solution.py
+++ b/solution.py
@@ -34,7 +34,7 @@
     F, RR, HB, VB, UF, RC, CC, CG, LT, SX, SXH, SXL, SY, SYT, SYH, SYL,
     P1, ZD, PC, ZC, EA, ER, TA, TR, AE,
     s_vb, s_f, s_rr, s_sx, s_sy, far_s, far_r, ys, yr, ds, dr, zd_s, zd_r, zc_s, zc_r, ea_s, ea_r, ta_s, ta_r,
-    x1, x2, y1, y2, zu, zd, go,
+    zu, zd, go,
 ):
     gy, gz = lax.axis_index("gy"), lax.axis_index("gz")
     x, zl, y = gy % NX, (gy // NX) % NZL, gy // (NX * NZL)
@@ -61,6 +61,44 @@
     for f, src in enumerate((fuel4, oxid4)):
         for j in range(4):
             pltpu.make_async_copy(src.at[:, j, :, plane(0), :], VB.at[:, :, f * 4 + j, :], s_vb).start()
+    barrier = pltpu.get_barrier_semaphore()
+    above, below = at(y, zl + 1, x), at(y, zl - 1, x)
+    rim_gz = 3 * (gz // 2)
+
+    for a in range(NY):
+        for b in range(NX):
+            device = {"gy": (((y + a) % NY) * NZL + zl) * NX + (x + b) % NX, "gz": rim_gz}
+            if a or b:
+                signal(barrier, device)
+
+    signal(barrier, partner)
+
+    @pl.when(inner)
+    def _():
+        signal(barrier, opposite)
+
+    @pl.when(rim)
+    def _():
+        @pl.when(zl < NZL - 1)
+        def _():
+            signal(barrier, above)
+
+        @pl.when(zl > 0)
+        def _():
+            signal(barrier, below)
+
+        UF[...] = jnp.zeros_like(UF)
+        ZC[...] = jnp.zeros_like(ZC)
+
+    @pl.when(gy == 0)
+    def _():
+        F[0] = jnp.zeros((NT, 8, 128), F32)
+
+    @pl.when(gy == DEVS - 1)
+    def _():
+        F[ROWS + 1] = jnp.zeros((NT, 8, 128), F32)
+
+    pltpu.make_async_copy(VB, VB, s_vb).wait()
     for f, src in enumerate((fuel, oxid)):
         for p in (3, 0, 1, 2):
             pltpu.make_async_copy(src.at[:, :, plane(p), :], F.at[pl.ds(1, ROWS), :, f * 4 + p, :], s_f).start()
@@ -70,56 +108,20 @@
     pltpu.make_async_copy(sx, SX, s_sx).start()
     pltpu.make_async_copy(sy, SY, s_sy).start()
 
-    barrier = pltpu.get_barrier_semaphore()
-    signal(barrier, partner)
-    right, left = at(y, zl, (x + 1) % NX), at(y, zl, (x + NX - 1) % NX)
-    front, back = at((y + 1) % NY, zl, x), at((y + NY - 1) % NY, zl, x)
-    above, below = at(y, zl + 1, x), at(y, zl - 1, x)
-
-    @pl.when(inner)
-    def _():
-        signal(barrier, opposite)
-
-    @pl.when(rim)
-    def _():
-        for device in (right, left, front, back):
-            signal(barrier, device)
-
-        @pl.when(zl < NZL - 1)
-        def _():
-            signal(barrier, above)
-
-        @pl.when(zl > 0)
-        def _():
-            signal(barrier, below)
-
-        UF[...] = jnp.zeros_like(UF)
-        ZC[...] = jnp.zeros_like(ZC)
-
-    @pl.when(gy == 0)
-    def _():
-        F[0] = jnp.zeros((NT, 8, 128), F32)
-
-    @pl.when(gy == DEVS - 1)
-    def _():
-        F[ROWS + 1] = jnp.zeros((NT, 8, 128), F32)
-
     @pl.when(inner)
     def _():
         pl.semaphore_wait(barrier, 2)
 
     @pl.when(rim & ((zl == 0) | (zl == NZL - 1)))
     def _():
-        pl.semaphore_wait(barrier, 6)
+        pl.semaphore_wait(barrier, 32)
 
     @pl.when(rim & (zl > 0) & (zl < NZL - 1))
     def _():
-        pl.semaphore_wait(barrier, 7)
+        pl.semaphore_wait(barrier, 33)
 
     def far(g):
         return remote(VB.at[g], UF.at[g], far_s.at[g], far_r.at[g], opposite)
-
-    pltpu.make_async_copy(VB, VB, s_vb).wait()
 
     @pl.when(inner)
     def _():
@@ -137,17 +139,6 @@
 
     @pl.when(rim)
     def _():
-        signal(x1, right)
-        signal(x1, left)
-        pl.semaphore_wait(x1, 2)
-        signal(x2, right)
-        pl.semaphore_wait(x2, 1)
-        signal(y1, front)
-        signal(y1, back)
-        pl.semaphore_wait(y1, 2)
-        signal(y2, front)
-        pl.semaphore_wait(y2, 1)
-
         @pl.when(zl == 0)
         def _():
             signal(zu, above)
@@ -179,6 +170,32 @@
             pl.semaphore_wait(zu, 1)
 
         signal(go, partner)
+
+    north = {"gy": gy + 1, "gz": gz}
+    south = {"gy": gy - 1, "gz": gz}
+
+    def to_north():
+        return remote(F.at[ROWS], F.at[0], ys.at[0], yr.at[0], north)
+
+    def to_south():
+        return remote(F.at[1], F.at[ROWS + 1], ys.at[1], yr.at[1], south)
+
+    def send_rows():
+        @pl.when(gy < DEVS - 1)
+        def _():
+            to_north().start()
+
+        @pl.when(gy > 0)
+        def _():
+            to_south().start()
+
+    @pl.when(gz == 1)
+    def _():
+        pl.semaphore_wait(go, 1)
+
+    @pl.when(gz != 2)
+    def _():
+        send_rows()
 
     sub = lax.broadcasted_iota(jnp.int32, (8, 128), 0)
     lane = lax.broadcasted_iota(jnp.int32, (8, 128), 1)
@@ -234,50 +251,21 @@
             total += dot(high, SXH[:, cols], nt) + dot(low, SXH[:, cols], nt) + dot(high, SXL[:, cols], nt)
         return total
 
-    P0 = project(lambda t: VB[:, t].reshape(32, 128), 32).reshape(4, 8, 128)
-
-    @pl.when(inner)
-    def _():
-        pl.semaphore_wait(go, 1)
-
-    north = {"gy": gy + 1, "gz": gz}
-    south = {"gy": gy - 1, "gz": gz}
-
-    def to_north():
-        return remote(F.at[ROWS], F.at[0], ys.at[0], yr.at[0], north)
-
-    def to_south():
-        return remote(F.at[1], F.at[ROWS + 1], ys.at[1], yr.at[1], south)
-
-    @pl.when(gy < DEVS - 1)
-    def _():
-        to_north().start()
-
-    @pl.when(gy > 0)
-    def _():
-        to_south().start()
-
     pltpu.make_async_copy(RR, RR, s_rr).wait()
     for f in range(2):
         deck(f).wait_recv()
 
-    @pl.when(gy > 0)
-    def _():
-        to_north().wait_recv()
-
-    @pl.when(gy < DEVS - 1)
-    def _():
-        to_south().wait_recv()
-
     @pl.loop(0, ROWS)
     def _(r):
+        kn, ks = jnp.where(r == ROWS - 1, zero, kN), jnp.where(r == 0, zero, kS)
+        rn, rs = jnp.minimum(r + 2, ROWS), jnp.maximum(r, 1)
         row = [F[r + 1, t] for t in range(NT)]
         ahead = along_x(row)
         after = []
         for t in range(NT):
             v = row[t]
             up = jnp.where(sp == 3, HB[r, t], roll(v, 7, 0))
-            c = ahead[t] + kN * F[r + 2, t] + kS * F[r, t] + kP * up + kMz * roll(v, 1, 0)
+            c = ahead[t] + kn * F[rn, t] + ks * F[rs, t] + kP * up + kMz * roll(v, 1, 0)
             c += sg * RR[r, t] * v * roll(v, 4, 0)
             CG[0, r, t] = c
             after.append(c)
@@ -285,30 +273,56 @@
             c = after[t]
             CG[1, r, t] = g + sgm * RR[r, t] * c * roll(c, 4, 0)
 
+    def to_partner():
+        return remote(P1, ZD, zd_s, zd_r, partner)
+
+    def to_opposite():
+        return remote(PC, ZC, zc_s, zc_r, opposite)
+
+    def compact_rows(g):
+        for t in range(NT):
+            CC[g, t] = compact([CG[0, 4 * g + j, t] for j in range(4)])
+
+    @pl.loop(0, 4)
+    def _(g):
+        compact_rows(g)
+        for t in range(NT):
+            RC[g, t] = compact([RR[4 * g + j, t] for j in range(4)])
+
+    local = project(lambda t: jnp.concatenate([VB[:, t].reshape(32, 128), CC[:, t].reshape(32, 128)], axis=0), 64)
+    P0 = local[:32].reshape(4, 8, 128)
+    PC[...] = local[32:].reshape(4, 8, 128)
+
+    @pl.when(inner)
+    def _():
+        to_opposite().start()
+
+    @pl.when(gz == 2)
+    def _():
+        pl.semaphore_wait(go, 1)
+        send_rows()
+
+    @pl.when(gy > 0)
+    def _():
+        to_north().wait_recv()
+
+    @pl.when(gy < DEVS - 1)
+    def _():
+        to_south().wait_recv()
+
+    for r, halo, k in ((0, 0, kS), (ROWS - 1, ROWS + 1, kN)):
+        after = [CG[0, r, t] + k * F[halo, t] for t in range(NT)]
+        for t, g in enumerate(along_x(after)):
+            c = after[t]
+            CG[0, r, t] = c
+            CG[1, r, t] = g + sgm * RR[r, t] * c * roll(c, 4, 0)
+    compact_rows(0)
+    compact_rows(3)
+
     early = project(lambda t: CG[:, :, t].reshape(256, 128), 256)
     P1[...] = early[:128].reshape(ROWS, 8, 128)
-    for g in range(4):
-        PC[g] = compact([P1[4 * g + j] for j in range(4)])
-
-    def to_partner():
-        return remote(P1, ZD, zd_s, zd_r, partner)
-
-    def to_opposite():
-        return remote(PC, ZC, zc_s, zc_r, opposite)
-
     to_partner().start()
-
-    @pl.when(inner)
-    def _():
-        to_opposite().start()
-
     Q = early[128:].reshape(ROWS, 8, 128)
-
-    @pl.loop(0, 4)
-    def _(g):
-        for t in range(NT):
-            CC[g, t] = compact([CG[0, 4 * g + j, t] for j in range(4)])
-            RC[g, t] = compact([RR[4 * g + j, t] for j in range(4)])
 
     to_partner().wait_recv()
     rows = []
@@ -323,10 +337,18 @@
     EA[...] = jnp.concatenate(rows, axis=0).T
 
     def exchange(src, dst, send, recv):
-        @pl.loop(1, DEVS)
-        def _(i):
-            to = lax.rem(gy + i, DEVS)
+        def one(to):
             remote(src.at[pl.ds(to, 1), :], dst.at[pl.ds(gy, 1), :], send, recv, {"gy": to, "gz": gz}).start()
+
+        @pl.loop(0, NZL)
+        def _(n):
+            zz = jnp.where(zl < NZL // 2, NZL - 1 - n, n)
+            for m in range(1, NX * NY):
+                one((((y + m // NX) % NY) * NZL + zz) * NX + (x + m % NX) % NX)
+
+            @pl.when(zz != zl)
+            def _():
+                one((y * NZL + zz) * NX + x)
 
         dst[pl.ds(gy, 1), :] = src[pl.ds(gy, 1), :]
 
@@ -361,8 +383,8 @@
         v += kN * jnp.where(sp == 3, ahead, roll(D[g], 7, 0))
         v += kS * jnp.where(sp == 0, behind, roll(D[g], 1, 0))
         X.append(v)
-    low_edge = kN * P1[0] + jnp.where(sp == 0, kN * D[0], zero)
-    high_edge = kS * P1[ROWS - 1] + jnp.where(sp == 0, kS * roll(D[3], 5, 0), zero)
+    low_edge = kN * P1[0] + jnp.where(sp == 0, 2.0 * kN * D[0], zero)
+    high_edge = kS * P1[ROWS - 1] + jnp.where(sp == 0, 2.0 * kS * roll(D[3], 5, 0), zero)
     spare = [low_edge, roll(low_edge, 2, 0), high_edge, roll(high_edge, 2, 0)] + [zero] * (ROWS - 4)
     rows = []
     for r in range(ROWS):
@@ -440,7 +462,7 @@
             vm(128, 128), vm(128, 128), vm(128, 128), vm(128, 128), vm(128, 128),
             dma, dma, dma, dma, dma, dma((4,)), dma((4,)), dma((2,)), dma((2,)), dma((2,)), dma((2,)),
             dma, dma, dma, dma, dma, dma, dma, dma,
-            one, one, one, one, one, one, one,
+            one, one, one,
         ],
         compiler_params=pltpu.CompilerParams(collective_id=0, has_side_effects=True),
         name="advect_sketch",

time: 58.8 us -> 52.1 us (0.89)
  Pallas kernels: 57.4 us -> 50.6 us
    pallas_call x1, Pallas kernels: 57.4 us -> 50.6 us  [per_device(): pl.pallas_call(kernel, out_shape=jax.ShapeDtypeStruct((1, 2, 4, 128), F32...]
where the time goes in v2:
time: 52.1 us; the launch traced here: 51.8 us
  Pallas kernels  50.6 us (97%)
  local copies, waits for them, and re-layouts  1.28 us (2%)
    pallas_call x1, Pallas kernels, per_device(): pl.pallas_call(kernel, out_shape=jax.ShapeDtypeStruct((1, 2, 4, 128), F32...  50.6 us
    unnamed x1, local copies, waits for them, and re-layouts  1.28 us

profile of v2, /device:TPU:1, one launch (start us, length us, event | category | flops | bytes accessed | tf_op | source)
XLA Modules:
  0.0 51.8 jit_solution(7596833110242077238)
XLA Ops:
  0.0 50.6 %advect_sketch.1 = f32[1,2,4,128]{3,2,1,0:T(4,128)} custom-call(f32[16,16,4,128]{3,2,1,0:T(4,128)} %bitcast.13, f32[4,4,16,4,128]{4,3,2,1,0:T(4,128)} %bitcast.14, f32[16,16,4,128]{3,2,1,0:T(4,128)} %bitcast.15, f32[4,4,16,4,128]{4,3,2,1,0:T(4,128)} %bitcast.16, f32[16,16,4,128]{3,2,1,0:T(4,128)} %bitcast.17, f32[3]{0:T(128)} %vel.1, f32[128,2048]{1,0:T(8,128)} %sx.1, ...), custom_call_target="tpu_custom_call" | custom-call | tf_op jit(solution)/shard_map/advect_sketch/pallas_call | solution.py:450
  50.6 1.3 %copy.8 = f32[1,2,4,128]{3,2,1,0:T(4,128)} copy(f32[1,2,4,128]{3,2,1,0:T(4,128)} %advect_sketch.1) | data formatting | bytes 8192

commit v3 on v2

--- a/solution.py
+++ b/solution.py
@@ -34,7 +34,7 @@
     F, RR, HB, VB, UF, RC, CC, CG, LT, SX, SXH, SXL, SY, SYT, SYH, SYL,
     P1, ZD, PC, ZC, EA, ER, TA, TR, AE,
     s_vb, s_f, s_rr, s_sx, s_sy, far_s, far_r, ys, yr, ds, dr, zd_s, zd_r, zc_s, zc_r, ea_s, ea_r, ta_s, ta_r,
-    zu, zd, go,
+    zu, zd, go, near, ready,
 ):
     gy, gz = lax.axis_index("gy"), lax.axis_index("gz")
     x, zl, y = gy % NX, (gy // NX) % NZL, gy // (NX * NZL)
@@ -73,7 +73,15 @@
 
     signal(barrier, partner)
 
-    @pl.when(inner)
+    @pl.when((x == NX - 1) & (gy < DEVS - 1))
+    def _():
+        signal(barrier, {"gy": gy + 1, "gz": rim_gz})
+
+    @pl.when((x == 0) & (gy > 0))
+    def _():
+        signal(barrier, {"gy": gy - 1, "gz": rim_gz})
+
+    @pl.when(gz == 1)
     def _():
         signal(barrier, opposite)
 
@@ -108,22 +116,27 @@
     pltpu.make_async_copy(sx, SX, s_sx).start()
     pltpu.make_async_copy(sy, SY, s_sy).start()
 
-    @pl.when(inner)
+    @pl.when(gz == 1)
+    def _():
+        pl.semaphore_wait(barrier, 1)
+
+    @pl.when(gz == 2)
     def _():
         pl.semaphore_wait(barrier, 2)
-
-    @pl.when(rim & ((zl == 0) | (zl == NZL - 1)))
-    def _():
-        pl.semaphore_wait(barrier, 32)
-
-    @pl.when(rim & (zl > 0) & (zl < NZL - 1))
-    def _():
-        pl.semaphore_wait(barrier, 33)
+        signal(ready, opposite)
+
+    ends = jnp.where((zl == 0) | (zl == NZL - 1), 32, 33)
+    ends += jnp.where((x == 0) & (gy > 0), 2, 0) + jnp.where((x == NX - 1) & (gy < DEVS - 1), 2, 0)
+
+    @pl.when(rim)
+    def _():
+        pl.semaphore_wait(barrier, ends)
+        signal(near, partner)
 
     def far(g):
         return remote(VB.at[g], UF.at[g], far_s.at[g], far_r.at[g], opposite)
 
-    @pl.when(inner)
+    @pl.when(gz == 2)
     def _():
         for g in range(4):
             far(g).start()
@@ -137,40 +150,6 @@
     for f in range(2):
         deck(f).start()
 
-    @pl.when(rim)
-    def _():
-        @pl.when(zl == 0)
-        def _():
-            signal(zu, above)
-
-        @pl.when(zl == NZL - 1)
-        def _():
-            signal(zd, below)
-
-        @pl.when((zl > 0) & (zl < NZL // 2))
-        def _():
-            pl.semaphore_wait(zu, 1)
-            signal(zu, above)
-            pl.semaphore_wait(zd, 1)
-            signal(zd, below)
-
-        @pl.when((zl < NZL - 1) & (zl >= NZL // 2))
-        def _():
-            pl.semaphore_wait(zd, 1)
-            signal(zd, below)
-            pl.semaphore_wait(zu, 1)
-            signal(zu, above)
-
-        @pl.when(zl == 0)
-        def _():
-            pl.semaphore_wait(zd, 1)
-
-        @pl.when(zl == NZL - 1)
-        def _():
-            pl.semaphore_wait(zu, 1)
-
-        signal(go, partner)
-
     north = {"gy": gy + 1, "gz": gz}
     south = {"gy": gy - 1, "gz": gz}
 
@@ -191,7 +170,7 @@
 
     @pl.when(gz == 1)
     def _():
-        pl.semaphore_wait(go, 1)
+        pl.semaphore_wait(near, 1)
 
     @pl.when(gz != 2)
     def _():
@@ -293,14 +272,54 @@
     P0 = local[:32].reshape(4, 8, 128)
     PC[...] = local[32:].reshape(4, 8, 128)
 
+    @pl.when(gz == 1)
+    def _():
+        pl.semaphore_wait(ready, 1)
+        for g in range(4):
+            far(g).start()
+
     @pl.when(inner)
     def _():
         to_opposite().start()
 
     @pl.when(gz == 2)
     def _():
-        pl.semaphore_wait(go, 1)
+        pl.semaphore_wait(near, 1)
         send_rows()
+
+    @pl.when(rim)
+    def _():
+        @pl.when(zl == 0)
+        def _():
+            signal(zu, above)
+
+        @pl.when(zl == NZL - 1)
+        def _():
+            signal(zd, below)
+
+        @pl.when((zl > 0) & (zl < NZL // 2))
+        def _():
+            pl.semaphore_wait(zu, 1)
+            signal(zu, above)
+            pl.semaphore_wait(zd, 1)
+            signal(zd, below)
+
+        @pl.when((zl < NZL - 1) & (zl >= NZL // 2))
+        def _():
+            pl.semaphore_wait(zd, 1)
+            signal(zd, below)
+            pl.semaphore_wait(zu, 1)
+            signal(zu, above)
+
+        @pl.when(zl == 0)
+        def _():
+            pl.semaphore_wait(zd, 1)
+
+        @pl.when(zl == NZL - 1)
+        def _():
+            pl.semaphore_wait(zu, 1)
+
+        signal(go, partner)
 
     @pl.when(gy > 0)
     def _():
@@ -354,6 +373,10 @@
 
     def all_rows(src, dst, send, recv):
         return remote(src.at[pl.ds(0, DEVS - 1), :], dst.at[pl.ds(0, DEVS - 1), :], send, recv, partner)
+
+    @pl.when(inner)
+    def _():
+        pl.semaphore_wait(go, 1)
 
     exchange(EA, ER, ea_s, ea_r)
 
@@ -462,7 +485,7 @@
             vm(128, 128), vm(128, 128), vm(128, 128), vm(128, 128), vm(128, 128),
             dma, dma, dma, dma, dma, dma((4,)), dma((4,)), dma((2,)), dma((2,)), dma((2,)), dma((2,)),
             dma, dma, dma, dma, dma, dma, dma, dma,
-            one, one, one,
+            one, one, one, one, one,
         ],
         compiler_params=pltpu.CompilerParams(collective_id=0, has_side_effects=True),
         name="advect_sketch",

time: 52.1 us -> 44.9 us (0.86)
  Pallas kernels: 50.6 us -> 43.4 us
    pallas_call x1, Pallas kernels: 50.6 us -> 43.4 us  [per_device(): pl.pallas_call(kernel, out_shape=jax.ShapeDtypeStruct((1, 2, 4, 128), F32...]
where the time goes in v3:
time: 44.9 us; the launch traced here: 44.7 us
  Pallas kernels  43.4 us (97%)
  local copies, waits for them, and re-layouts  1.28 us (3%)
    pallas_call x1, Pallas kernels, per_device(): pl.pallas_call(kernel, out_shape=jax.ShapeDtypeStruct((1, 2, 4, 128), F32...  43.4 us
    unnamed x1, local copies, waits for them, and re-layouts  1.28 us

profile of v3, /device:TPU:1, one launch (start us, length us, event | category | flops | bytes accessed | tf_op | source)
XLA Modules:
  0.0 44.7 jit_solution(11066579322503447934)
XLA Ops:
  0.0 43.4 %advect_sketch.1 = f32[1,2,4,128]{3,2,1,0:T(4,128)} custom-call(f32[16,16,4,128]{3,2,1,0:T(4,128)} %bitcast.13, f32[4,4,16,4,128]{4,3,2,1,0:T(4,128)} %bitcast.14, f32[16,16,4,128]{3,2,1,0:T(4,128)} %bitcast.15, f32[4,4,16,4,128]{4,3,2,1,0:T(4,128)} %bitcast.16, f32[16,16,4,128]{3,2,1,0:T(4,128)} %bitcast.17, f32[3]{0:T(128)} %vel.1, f32[128,2048]{1,0:T(8,128)} %sx.1, ...), custom_call_target="tpu_custom_call" | custom-call | tf_op jit(solution)/shard_map/advect_sketch/pallas_call | solution.py:473
  43.4 1.3 %copy.8 = f32[1,2,4,128]{3,2,1,0:T(4,128)} copy(f32[1,2,4,128]{3,2,1,0:T(4,128)} %advect_sketch.1) | data formatting | bytes 8192

commit v4 on v3

--- a/solution.py
+++ b/solution.py
@@ -32,7 +32,7 @@
 def kernel(
     fuel, fuel4, oxid, oxid4, rate, vel, sx, sy, out,
     F, RR, HB, VB, UF, RC, CC, CG, LT, SX, SXH, SXL, SY, SYT, SYH, SYL,
-    P1, ZD, PC, ZC, EA, ER, TA, TR, AE,
+    P1, QM, ZD, PC, ZC, EA, ER, TA, TR, AE,
     s_vb, s_f, s_rr, s_sx, s_sy, far_s, far_r, ys, yr, ds, dr, zd_s, zd_r, zc_s, zc_r, ea_s, ea_r, ta_s, ta_r,
     zu, zd, go, near, ready,
 ):
@@ -132,6 +132,14 @@
     def _():
         pl.semaphore_wait(barrier, ends)
         signal(near, partner)
+
+        @pl.when(zl == 0)
+        def _():
+            signal(zu, above)
+
+        @pl.when(zl == NZL - 1)
+        def _():
+            signal(zd, below)
 
     def far(g):
         return remote(VB.at[g], UF.at[g], far_s.at[g], far_r.at[g], opposite)
@@ -227,7 +235,8 @@
             high, low = split(jnp.concatenate([read(2 * c), read(2 * c + 1)], axis=1))
             cols = slice(c * 256, (c + 1) * 256)
             nt = ((1,), (1,))
-            total += dot(high, SXH[:, cols], nt) + dot(low, SXH[:, cols], nt) + dot(high, SXL[:, cols], nt)
+            both = dot(jnp.concatenate([high, low], axis=0), SXH[:, cols], nt)
+            total += both[:rows] + both[rows:] + dot(high, SXL[:, cols], nt)
         return total
 
     pltpu.make_async_copy(RR, RR, s_rr).wait()
@@ -275,10 +284,11 @@
     @pl.when(gz == 1)
     def _():
         pl.semaphore_wait(ready, 1)
+        to_opposite().start()
         for g in range(4):
             far(g).start()
 
-    @pl.when(inner)
+    @pl.when(gz == 2)
     def _():
         to_opposite().start()
 
@@ -287,16 +297,13 @@
         pl.semaphore_wait(near, 1)
         send_rows()
 
+    middle = (ROWS - 2) * 8
+    early = project(lambda t: CG[:, 1 : ROWS - 1, t].reshape(2 * middle, 128), 2 * middle)
+    P1[1 : ROWS - 1] = early[:middle].reshape(ROWS - 2, 8, 128)
+    QM[...] = early[middle:].reshape(ROWS - 2, 8, 128)
+
     @pl.when(rim)
     def _():
-        @pl.when(zl == 0)
-        def _():
-            signal(zu, above)
-
-        @pl.when(zl == NZL - 1)
-        def _():
-            signal(zd, below)
-
         @pl.when((zl > 0) & (zl < NZL // 2))
         def _():
             pl.semaphore_wait(zu, 1)
@@ -338,10 +345,13 @@
     compact_rows(0)
     compact_rows(3)
 
-    early = project(lambda t: CG[:, :, t].reshape(256, 128), 256)
-    P1[...] = early[:128].reshape(ROWS, 8, 128)
+    brims = project(
+        lambda t: jnp.concatenate([CG[0, 0, t], CG[0, ROWS - 1, t], CG[1, 0, t], CG[1, ROWS - 1, t]], axis=0), 32
+    )
+    P1[0] = brims[:8]
+    P1[ROWS - 1] = brims[8:16]
     to_partner().start()
-    Q = early[128:].reshape(ROWS, 8, 128)
+    Q = [brims[16:24]] + [QM[r] for r in range(ROWS - 2)] + [brims[24:]]
 
     to_partner().wait_recv()
     rows = []
@@ -429,7 +439,8 @@
     A[0] += jnp.where(first, zero, roll(high_edge, 1, 1))
     high, low = split(jnp.concatenate(A, axis=1))
     nn = ((1,), (0,))
-    res = dot(high, SYH[...], nn) + dot(low, SYH[...], nn) + dot(high, SYL[...], nn)
+    both = dot(jnp.concatenate([high, low], axis=0), SYH[...], nn)
+    res = both[:8] + both[8:] + dot(high, SYL[...], nn)
     flipped = jnp.where(
         sp == 0, roll(res, 5, 0), jnp.where(sp == 1, roll(res, 7, 0), jnp.where(sp == 2, roll(res, 1, 0), roll(res, 3, 0)))
     )
@@ -481,7 +492,7 @@
             vm(ROWS + 2, NT, 8, 128), vm(*whole), vm(*whole), vm(*plane), vm(*plane), vm(*plane), vm(*plane),
             vm(2, *whole), vm(8, NT, 8, 128), vm(128, 2048), vm(128, 2048, kind=BF16), vm(128, 2048, kind=BF16),
             vm(128, 2048), vm(2048, 128), vm(2048, 128, kind=BF16), vm(2048, 128, kind=BF16),
-            vm(ROWS, 8, 128), vm(ROWS, 8, 128), vm(4, 8, 128), vm(4, 8, 128),
+            vm(ROWS, 8, 128), vm(ROWS - 2, 8, 128), vm(ROWS, 8, 128), vm(4, 8, 128), vm(4, 8, 128),
             vm(128, 128), vm(128, 128), vm(128, 128), vm(128, 128), vm(128, 128),
             dma, dma, dma, dma, dma, dma((4,)), dma((4,)), dma((2,)), dma((2,)), dma((2,)), dma((2,)),
             dma, dma, dma, dma, dma, dma, dma, dma,

time: 44.9 us -> 44.7 us (level)
  no operation moved by 1% of the time
where the time goes in v4:
time: 44.7 us; the launch traced here: 44.4 us
  Pallas kernels  43.2 us (97%)
  local copies, waits for them, and re-layouts  1.28 us (3%)
    pallas_call x1, Pallas kernels, per_device(): pl.pallas_call(kernel, out_shape=jax.ShapeDtypeStruct((1, 2, 4, 128), F32...  43.2 us
    unnamed x1, local copies, waits for them, and re-layouts  1.28 us

profile of v4, /device:TPU:1, one launch (start us, length us, event | category | flops | bytes accessed | tf_op | source)
XLA Modules:
  0.0 44.4 jit_solution(10228219156012956296)
XLA Ops:
  0.0 43.2 %advect_sketch.1 = f32[1,2,4,128]{3,2,1,0:T(4,128)} custom-call(f32[16,16,4,128]{3,2,1,0:T(4,128)} %bitcast.13, f32[4,4,16,4,128]{4,3,2,1,0:T(4,128)} %bitcast.14, f32[16,16,4,128]{3,2,1,0:T(4,128)} %bitcast.15, f32[4,4,16,4,128]{4,3,2,1,0:T(4,128)} %bitcast.16, f32[16,16,4,128]{3,2,1,0:T(4,128)} %bitcast.17, f32[3]{0:T(128)} %vel.1, f32[128,2048]{1,0:T(8,128)} %sx.1, ...), custom_call_target="tpu_custom_call" | custom-call | tf_op jit(solution)/shard_map/advect_sketch/pallas_call | solution.py:484
  43.2 1.3 %copy.8 = f32[1,2,4,128]{3,2,1,0:T(4,128)} copy(f32[1,2,4,128]{3,2,1,0:T(4,128)} %advect_sketch.1) | data formatting | bytes 8192

commit v5 on v4

--- a/solution.py
+++ b/solution.py
@@ -372,12 +372,12 @@
         @pl.loop(0, NZL)
         def _(n):
             zz = jnp.where(zl < NZL // 2, NZL - 1 - n, n)
-            for m in range(1, NX * NY):
-                one((((y + m // NX) % NY) * NZL + zz) * NX + (x + m % NX) % NX)
-
-            @pl.when(zz != zl)
-            def _():
-                one((y * NZL + zz) * NX + x)
+            for m in range(NX * NY):
+                to = ((m // NX) * NZL + zz) * NX + m % NX
+
+                @pl.when(to != gy)
+                def _():
+                    one(to)
 
         dst[pl.ds(gy, 1), :] = src[pl.ds(gy, 1), :]
 

time: 44.7 us -> 44.6 us (level)
  no operation moved by 1% of the time
where the time goes in v5:
time: 44.6 us; the launch traced here: 44.4 us
  Pallas kernels  43.1 us (97%)
  local copies, waits for them, and re-layouts  1.28 us (3%)
    pallas_call x1, Pallas kernels, per_device(): pl.pallas_call(kernel, out_shape=jax.ShapeDtypeStruct((1, 2, 4, 128), F32...  43.1 us
    unnamed x1, local copies, waits for them, and re-layouts  1.28 us

profile of v5, /device:TPU:1, one launch (start us, length us, event | category | flops | bytes accessed | tf_op | source)
XLA Modules:
  0.0 44.4 jit_solution(15203909348009676220)
XLA Ops:
  0.0 43.1 %advect_sketch.1 = f32[1,2,4,128]{3,2,1,0:T(4,128)} custom-call(f32[16,16,4,128]{3,2,1,0:T(4,128)} %bitcast.13, f32[4,4,16,4,128]{4,3,2,1,0:T(4,128)} %bitcast.14, f32[16,16,4,128]{3,2,1,0:T(4,128)} %bitcast.15, f32[4,4,16,4,128]{4,3,2,1,0:T(4,128)} %bitcast.16, f32[16,16,4,128]{3,2,1,0:T(4,128)} %bitcast.17, f32[3]{0:T(128)} %vel.1, f32[128,2048]{1,0:T(8,128)} %sx.1, ...), custom_call_target="tpu_custom_call" | custom-call | tf_op jit(solution)/shard_map/advect_sketch/pallas_call | solution.py:484
  43.1 1.3 %copy.8 = f32[1,2,4,128]{3,2,1,0:T(4,128)} copy(f32[1,2,4,128]{3,2,1,0:T(4,128)} %advect_sketch.1) | data formatting | bytes 8192
